TPU v7x, 32 devices: a whole 2x2x4 slice. The times are simulated.
32 devices in a mesh: gx: 4 (over y, x), gy: 8 (over z, core).
Axes of the slice: x: 2, y: 2, z: 4, core: 2. Of those that a mesh axis runs over, the one named last changes fastest.
Arguments:
- facets: float32 [2048, 12, 128], P(('gx', 'gy')), may hold values from -6 to 6
- owner: int32 [2048, 1], P(('gx', 'gy')), may hold values from 0 to 31; in each aligned block of 64 rows (0 to 63, 64 to 127, ...) at most 4 rows name the same one
- ghosts: int32 [32, 16], P(('gx', 'gy')), may hold values from 0 to 2047, as said below
- ghost_count: int32 [32], P(('gx', 'gy')), may hold values from 1 to 16, 256 in all
- nodes: float32 [3, 16384], P(None, ('gx', 'gy')), may hold values from -6 to 6
- cand: int32 [4, 16384], P(None, ('gx', 'gy')), may hold values from 0 to 15
Outputs:
- own_gap: float32 [16384], P(('gx', 'gy'))
- ghost_gap: float32 [16384], P(('gx', 'gy'))
Inputs may be any that keep to these rules, and one draw needn't show every extreme that they name: Among the 64 blocks of one element-order device at most 4 have the same owner, and some owner reaches 4; every partition owns at least one block. `ghosts`: each row holds 16 distinct block ids. The blocks of element-order device h are h * 64 to h * 64 + 63; in every row exactly one device holds 2 of the entries and every other device holds at most one.
All inputs are finite; a program needn't handle non-finite values. No bound on the sum of `ghost_count` on one device may be relied on, other than what follows from the above.
Results may differ from a plain program's by a relative error of at most 0.0003.
Values sent between devices are 32-bit elements; how exact they have to be, the bound alone decides.
A program may use at most 64 MiB of HBM per device.

v0:
```python
import math

import jax
import jax.numpy as jnp
from jax import lax
from jax.sharding import PartitionSpec as P

CAP = 4
GC = 2


far_gap = 10.0
penalty = 1e30


def facet_features(blocks, absent):
    vertex_a = blocks[:, 0:3]
    vertex_b = blocks[:, 3:6]
    vertex_c = blocks[:, 6:9]
    normal = blocks[:, 9:12]
    centre = (vertex_a + vertex_b + vertex_c) / 3.0
    spread = jnp.sum(vertex_a * vertex_a + vertex_b * vertex_b + vertex_c * vertex_c, axis=1) / 3.0
    offset = spread - jnp.sum(normal * vertex_a, axis=1) + penalty * absent[:, None]
    linear = normal - 2.0 * centre
    unit_row = jnp.ones_like(offset)
    stacked = jnp.concatenate([linear, unit_row[:, None], offset[:, None]], axis=1)
    return jnp.moveaxis(stacked, 1, 0).reshape(5, -1)


def node_features(points):
    square = jnp.sum(points * points, axis=0, keepdims=True)
    return jnp.concatenate([points, square, jnp.ones_like(square)], axis=0)


def pair_gaps(node_feat, facet_feat):
    return lax.dot_general(
        node_feat,
        facet_feat,
        (((0,), (0,)), ((), ())),
        precision=lax.Precision.HIGHEST,
        preferred_element_type=jnp.float32,
    )


def local(facets, owner, ghosts, ghost_count, nodes, cand):
    part_count = lax.axis_size(("gx", "gy"))
    blocks_dev = facets.shape[0]
    facet_width = facets.shape[2]
    nodes_dev = nodes.shape[1]
    capacity = CAP
    pair_slots = GC
    slot_count = part_count * capacity
    target = owner[:, 0]
    node_feat = node_features(nodes)
    position = jnp.arange(blocks_dev, dtype=jnp.int32)
    before = (target[:, None] == target[None, :]) & (position[None, :] < position[:, None])
    rank_in = jnp.sum(before.astype(jnp.int32), axis=1, dtype=jnp.int32)
    slot_of = target * capacity + rank_in
    outgoing = jnp.zeros((slot_count, 12, facet_width), jnp.float32).at[slot_of].set(facets)
    present = jnp.zeros((slot_count,), jnp.float32).at[slot_of].set(1.0)
    arrived, arrival_flags = (
        lax.all_to_all(
            outgoing.reshape(part_count, capacity, 12, facet_width),
            ("gx", "gy"),
            split_axis=0,
            concat_axis=0,
            tiled=True,
        ),
        lax.all_to_all(
            present.reshape(part_count, capacity),
            ("gx", "gy"),
            split_axis=0,
            concat_axis=0,
            tiled=True,
        ),
    )
    arrived = arrived.reshape(slot_count, 12, facet_width)
    absent = 1.0 - arrival_flags.reshape(slot_count)
    group_size = math.gcd(32, slot_count)
    rounds = slot_count // group_size

    def own_step(running, operands):
        pieces, missing = operands
        gap_block = pair_gaps(node_feat, facet_features(pieces, missing))
        return (jnp.minimum(running, jnp.min(gap_block, axis=1)), None)

    initial = jnp.full((nodes_dev,), penalty, jnp.float32)
    own_gap, unused = lax.scan(
        own_step,
        initial,
        (arrived.reshape(rounds, group_size, 12, facet_width), absent.reshape(rounds, group_size)),
    )
    wanted = ghosts[0]
    holder = wanted // blocks_dev
    local_row = wanted % blocks_dev
    entries = jnp.arange(wanted.shape[0], dtype=jnp.int32)
    slot_ids = jnp.arange(pair_slots, dtype=jnp.int32)
    earlier = (holder[:, None] == holder[None, :]) & (entries[None, :] < entries[:, None])
    order_in = jnp.sum(earlier.astype(jnp.int32), axis=1, dtype=jnp.int32)
    all_parts = jnp.arange(part_count, dtype=jnp.int32)
    select = (holder[None, None, :] == all_parts[:, None, None]) & (
        order_in[None, None, :] == slot_ids[None, :, None]
    )
    request = jnp.sum(select.astype(jnp.int32) * local_row[None, None, :], axis=2, dtype=jnp.int32)
    reply = lax.all_to_all(
        facets[lax.all_to_all(request, ("gx", "gy"), split_axis=0, concat_axis=0, tiled=True)],
        ("gx", "gy"),
        split_axis=0,
        concat_axis=0,
        tiled=True,
    )
    fetched = reply[holder, order_in]
    ghost_feat = facet_features(fetched, jnp.zeros((fetched.shape[0],), jnp.float32))
    gap_block = pair_gaps(node_feat, ghost_feat).reshape(nodes_dev, fetched.shape[0], facet_width)
    limit = ghost_count[0]
    active = jnp.any(
        (cand[:, :, None] == entries[None, None, :]) & (entries[None, None, :] < limit), axis=0
    )
    ghost_gap = jnp.minimum(
        far_gap, jnp.min(jnp.where(active[:, :, None], gap_block, penalty), axis=(1, 2))
    )
    return (own_gap, ghost_gap)


def solution(mesh):
    return jax.shard_map(
        local,
        mesh=mesh,
        in_specs=(
            P(("gx", "gy"), None, None),
            P(("gx", "gy"), None),
            P(("gx", "gy"), None),
            P(("gx", "gy")),
            P(None, ("gx", "gy")),
            P(None, ("gx", "gy")),
        ),
        out_specs=(P(("gx", "gy")), P(("gx", "gy"))),
        check_vma=False,
    )
```

profile of v0, /device:TPU:0, one launch (start us, length us, event | category | flops | bytes accessed | tf_op | source)
XLA Modules:
  0.0 99.3 jit_solution(10819551516194898591)
XLA Ops:
  0.6 0.7 and_select_fusion.3
  1.3 0.7 fusion.20
  2.0 0.1 iota_compare_fusion.3
  2.0 0.2 convert_reduce_fusion.1
  2.2 0.1 select_reduce_fusion.1
  2.3 0.7 copy.35
  3.0 7.3 %all-to-all-start.2 = ((s32[32,1,2]{2,1,0:T(1,128)}), s32[32,1,2]{2,1,0:T(1,128)S(1)}, u32[]{:S(2)}, u32[]{:S(2)}) async-start(s32[32,1,2]{2,1,0:T(1,128)} %copy.35), calls=%async_computation.2 | async-start | bytes 32768 | tf_op jit(solution)/shard_map/all_to_all | solution.py:106
  10.3 0.9 convert_reduce_fusion
  11.3 0.7 fusion.14
  11.9 0.8 scatter_custom_fusion.1
  12.7 0.7 all_to_all.21
  13.4 4.1 %all-to-all-done.2 = s32[32,1,2]{2,1,0:T(1,128)S(1)} async-done(((s32[32,1,2]{2,1,0:T(1,128)}), s32[32,1,2]{2,1,0:T(1,128)S(1)}, u32[]{:S(2)}, u32[]{:S(2)}) %all-to-all-start.2) | async-done | bytes 288 | tf_op jit(solution)/shard_map/all_to_all | solution.py:106
  17.5 2.6 %all-to-all-start.1 = ((f32[32,1,4]{2,1,0:T(1,128)}), f32[32,1,4]{2,1,0:T(1,128)S(1)}, u32[]{:S(2)}, u32[]{:S(2)}) async-start(f32[32,1,4]{2,1,0:T(1,128)} %bitcast.5), calls=%async_computation.1 | async-start | bytes 32768 | tf_op jit(solution)/shard_map/all_to_all | solution.py:69
  20.1 0.1 copy.36
  20.2 0.1 copy.37
  20.3 0.1 reshape.343
  20.4 2.3 %gather_fusion = f32[64,12,128]{2,0,1:T(8,128)S(1)} fusion(f32[64,12,128]{2,0,1:T(8,128)} %param.8, s32[1024]{0:T(1024)S(1)} %pad_clamp_fusion), kind=kCustom, calls=%fused_computation | custom fusion | bytes 786688 | tf_op jit(solution)/shard_map/gather | solution.py:106
  22.7 0.0 copy-start
  22.7 0.9 copy.38
  23.6 3.7 %all-to-all-done.1 = f32[32,1,4]{2,1,0:T(1,128)S(1)} async-done(((f32[32,1,4]{2,1,0:T(1,128)}), f32[32,1,4]{2,1,0:T(1,128)S(1)}, u32[]{:S(2)}, u32[]{:S(2)}) %all-to-all-start.1) | async-done | bytes 544 | tf_op jit(solution)/shard_map/all_to_all | solution.py:69
  27.3 2.6 %all-to-all-start.3 = ((f32[32,2,12,128]{3,1,2,0:T(2,128)}), f32[32,2,12,128]{3,1,2,0:T(2,128)S(1)}, u32[]{:S(2)}, u32[]{:S(2)}) async-start(f32[32,2,12,128]{3,1,2,0:T(2,128)} %copy.38), calls=%async_computation.3 | async-start | bytes 786432 | tf_op jit(solution)/shard_map/all_to_all | solution.py:105
  29.9 0.0 copy-done
  29.9 0.2 copy.30
  30.1 0.1 pad.8.clone
  30.2 0.1 pad.4.clone
  30.3 0.1 broadcast_in_dim.23
  30.3 2.4 %scatter_fusion = f32[128,12,128]{2,1,0:T(8,128)S(1)} fusion(f32[128,12,128]{2,1,0:T(8,128)S(1)} %broadcast_in_dim.23, s32[64]{0:T(128)S(1)} %fusion.14, f32[64,12,128]{2,1,0:T(8,128)S(1)} %copy.30), kind=kCustom, calls=%fused_computation.2 | custom fusion | bytes 1179904 | tf_op jit(solution)/shard_map/scatter | solution.py:59
  32.8 0.0 copy-start.3
  32.8 1.2 %copy.31 = f32[32,4,12,128]{3,1,2,0:T(4,128)} copy(f32[32,4,12,128]{3,2,1,0:T(8,128)S(1)} %bitcast.95) | data formatting | bytes 1572864 | tf_op jit(solution)/shard_map/reshape | solution.py:63
  34.7 0.1 fusion.6
  34.8 8.5 %all-to-all-done.3 = f32[32,2,12,128]{3,1,2,0:T(2,128)S(1)} async-done(((f32[32,2,12,128]{3,1,2,0:T(2,128)}), f32[32,2,12,128]{3,1,2,0:T(2,128)S(1)}, u32[]{:S(2)}, u32[]{:S(2)}) %all-to-all-start.3) | async-done | bytes 393248 | tf_op jit(solution)/shard_map/all_to_all | solution.py:105
  43.3 2.6 %all-to-all-start = ((f32[32,4,12,128]{3,1,2,0:T(4,128)}), f32[32,4,12,128]{3,1,2,0:T(4,128)S(1)}, u32[]{:S(2)}, u32[]{:S(2)}) async-start(f32[32,4,12,128]{3,1,2,0:T(4,128)} %copy.31), calls=%async_computation | async-start | bytes 1572864 | tf_op jit(solution)/shard_map/all_to_all | solution.py:62
  46.0 0.1 maximum_maximum_fusion
  46.1 0.1 sub.58
  46.2 0.1 copy.39
  46.3 0.6 gather_fusion.1
  46.9 0.1 add_reduce_fusion.1
  47.0 3.9 %select_reduce_fusion = f32[512]{0:T(512)S(1)} fusion(pred[512,16]{0,1:T(8,128)(4,1)S(1)} %fusion.6, f32[16,1,128]{2,1,0:T(1,128)S(1)} %bitcast.99, f32[16,3,128]{2,1,0:T(4,128)S(1)} %get-tuple-element.111, f32[5]{0:T(128)S(1)} %pad.4.clone, f32[1,512]{1,0:T(1,128)S(1)} %bitcast.101, f32[3,512]{1,0:T(4,128)S(1)} %copy-done.2, f32[5]{0:T(128)S(1)} %pad.8.clone), kind=kOutput, calls=%fused_computation.20 | convolution fusion | flops 65036800 | bytes 51240 | tf_op jit(solution)/shard_map/dot_general | solution.py:36
  50.9 0.6 broadcast_minimum_fusion
  51.5 16.3 %all-to-all-done = f32[32,4,12,128]{3,1,2,0:T(4,128)S(1)} async-done(((f32[32,4,12,128]{3,1,2,0:T(4,128)}), f32[32,4,12,128]{3,1,2,0:T(4,128)S(1)}, u32[]{:S(2)}, u32[]{:S(2)}) %all-to-all-start) | async-done | bytes 786464 | tf_op jit(solution)/shard_map/all_to_all | solution.py:62
  67.8 0.2 copy.32
  68.0 30.7 %while.13 = (s32[]{:T(128)}, f32[512]{0:T(512)S(1)}, f32[4,32,12,128]{3,1,0,2:T(8,128)S(1)}, f32[4,32]{1,0:T(4,128)S(1)}, f32[5,512]{1,0:T(8,128)S(1)}, /*index=5*/s32[]{:T(128)}, f32[]{:T(128)}, f32[]{:T(128)}, s32[]{:T(128)}) while((s32[]{:T(128)}, f32[512]{0:T(512)S(1)}, f32[4,32,12,128]{3,1,0,2:T(8,128)S(1)}, ...), condition=%wide.region_8.9_spmd.clone, body=%wide.region_4.8_spmd.clone.sunk | while | flops 128119328 | bytes 1231399 | solution.py:88
  68.0 0.1 copy.44
  68.1 0.1 add_reduce_fusion.3
  68.3 0.1 broadcast_add_fusion.2
  68.4 0.1 pad.1.clone.2
  68.5 7.1 %convolution_reduce_fusion.2 = f32[512]{0:T(512)S(1)} fusion(f32[5,512]{1,0:T(8,128)S(1)} %get-tuple-element.173, f32[32,1,128]{2,1,0:T(1,128)S(1)} %broadcast_add_fusion.2, f32[32,3,128]{2,1,0:T(4,128)S(1)} %get-tuple-element.150, f32[5]{0:T(128)S(1)} %pad.1.clone.2), kind=kOutput, calls=%fused_computation.4.clone.1 | convolution fusion | flops 127966720 | bytes 77844 | tf_op jit(solution)/shard_map/while/body/eval_jaxpr/dot_general | solution.py:36
  75.7 0.1 copy.44
  75.8 0.1 add_reduce_fusion.3
  76.0 0.1 broadcast_add_fusion.2
  76.1 0.1 pad.1.clone.2
  76.2 7.1 %convolution_reduce_fusion.2 = f32[512]{0:T(512)S(1)} fusion(f32[5,512]{1,0:T(8,128)S(1)} %get-tuple-element.173, f32[32,1,128]{2,1,0:T(1,128)S(1)} %broadcast_add_fusion.2, f32[32,3,128]{2,1,0:T(4,128)S(1)} %get-tuple-element.150, f32[5]{0:T(128)S(1)} %pad.1.clone.2), kind=kOutput, calls=%fused_computation.4.clone.1 | convolution fusion | flops 127966720 | bytes 77844 | tf_op jit(solution)/shard_map/while/body/eval_jaxpr/dot_general | solution.py:36
  83.4 0.1 copy.44
  83.5 0.1 add_reduce_fusion.3
  83.7 0.1 broadcast_add_fusion.2
  83.8 0.1 pad.1.clone.2
  83.8 7.1 %convolution_reduce_fusion.2 = f32[512]{0:T(512)S(1)} fusion(f32[5,512]{1,0:T(8,128)S(1)} %get-tuple-element.173, f32[32,1,128]{2,1,0:T(1,128)S(1)} %broadcast_add_fusion.2, f32[32,3,128]{2,1,0:T(4,128)S(1)} %get-tuple-element.150, f32[5]{0:T(128)S(1)} %pad.1.clone.2), kind=kOutput, calls=%fused_computation.4.clone.1 | convolution fusion | flops 127966720 | bytes 77844 | tf_op jit(solution)/shard_map/while/body/eval_jaxpr/dot_general | solution.py:36
  91.0 0.1 copy.44
  91.2 0.1 add_reduce_fusion.3
  91.3 0.1 broadcast_add_fusion.2
  91.4 0.1 pad.1.clone.2
  91.5 7.1 %convolution_reduce_fusion.2 = f32[512]{0:T(512)S(1)} fusion(f32[5,512]{1,0:T(8,128)S(1)} %get-tuple-element.173, f32[32,1,128]{2,1,0:T(1,128)S(1)} %broadcast_add_fusion.2, f32[32,3,128]{2,1,0:T(4,128)S(1)} %get-tuple-element.150, f32[5]{0:T(128)S(1)} %pad.1.clone.2), kind=kOutput, calls=%fused_computation.4.clone.1 | convolution fusion | flops 127966720 | bytes 77844 | tf_op jit(solution)/shard_map/while/body/eval_jaxpr/dot_general | solution.py:36
  98.7 0.0 copy-start.1
  98.7 0.6 copy-done.1
  (31 shorter events, 0.3 us)
Async XLA Ops:
  3.0 14.5 %all-to-all-start.2 = ((s32[32,1,2]{2,1,0:T(1,128)}), s32[32,1,2]{2,1,0:T(1,128)S(1)}, u32[]{:S(2)}, u32[]{:S(2)}) async-start(s32[32,1,2]{2,1,0:T(1,128)} %copy.35), calls=%async_computation.2 | async-start | bytes 32768 | tf_op jit(solution)/shard_map/all_to_all | solution.py:106
  17.5 9.7 %all-to-all-start.1 = ((f32[32,1,4]{2,1,0:T(1,128)}), f32[32,1,4]{2,1,0:T(1,128)S(1)}, u32[]{:S(2)}, u32[]{:S(2)}) async-start(f32[32,1,4]{2,1,0:T(1,128)} %bitcast.5), calls=%async_computation.1 | async-start | bytes 32768 | tf_op jit(solution)/shard_map/all_to_all | solution.py:69
  22.7 7.2 %copy-start = (f32[64,12,128]{2,0,1:T(8,128)S(1)}, f32[64,12,128]{2,0,1:T(8,128)}, u32[]{:S(2)}) copy-start(f32[64,12,128]{2,0,1:T(8,128)} %param.8) | copy-start | bytes 1179652
  27.3 16.0 %all-to-all-start.3 = ((f32[32,2,12,128]{3,1,2,0:T(2,128)}), f32[32,2,12,128]{3,1,2,0:T(2,128)S(1)}, u32[]{:S(2)}, u32[]{:S(2)}) async-start(f32[32,2,12,128]{3,1,2,0:T(2,128)} %copy.38), calls=%async_computation.3 | async-start | bytes 786432 | tf_op jit(solution)/shard_map/all_to_all | solution.py:105
  32.8 1.9 %copy-start.3 = (s32[4,512]{1,0:T(4,128)S(1)}, s32[4,512]{1,0:T(4,128)}, u32[]{:S(2)}) copy-start(s32[4,512]{1,0:T(4,128)} %param.13) | copy-start | bytes 24580
  34.0 11.9 %copy-start.2 = (f32[3,512]{1,0:T(4,128)S(1)}, f32[3,512]{1,0:T(4,128)}, u32[]{:S(2)}) copy-start(f32[3,512]{1,0:T(4,128)} %param.12) | copy-start | bytes 18436
  34.0 12.0 %copy-start.4 = (s32[1,16]{1,0:T(1,128)S(1)}, s32[1,16]{1,0:T(1,128)}, u32[]{:S(2)}) copy-start(s32[1,16]{1,0:T(1,128)} %param.10) | copy-start | bytes 196
  43.3 24.5 %all-to-all-start = ((f32[32,4,12,128]{3,1,2,0:T(4,128)}), f32[32,4,12,128]{3,1,2,0:T(4,128)S(1)}, u32[]{:S(2)}, u32[]{:S(2)}) async-start(f32[32,4,12,128]{3,1,2,0:T(4,128)} %copy.31), calls=%async_computation | async-start | bytes 1572864 | tf_op jit(solution)/shard_map/all_to_all | solution.py:62
  98.7 0.6 copy-start.1
where the time goes:
time: 99.7 us; the launch traced here: 99.3 us
  waiting for transfers between devices  32.6 us (33%)
  matrix products  32.4 us (32%)
  starting transfers between devices  15.1 us (15%)
  local copies, waits for them, and re-layouts  12.1 us (12%)
  other arithmetic  5.25 us (5%)
  between operations  1.54 us (2%)
    dot_general x5, matrix products, pair_gaps(): lax.dot_general(node_feat, facet_feat, (((0,), (0,)), ((), ())), precisio...  32.4 us
    all_to_all x1, waiting for transfers between devices, local(): lax.all_to_all(outgoing.reshape(part_count, capacity, 12, facet_width), (...  16.3 us
    all_to_all x1, waiting for transfers between devices, local(): lax.all_to_all(facets[lax.all_to_all(request, ('gx', 'gy'), split_axis=0,...  8.5 us
    all_to_all x1, starting transfers between devices, local(): lax.all_to_all(request, ('gx', 'gy'), split_axis=0, concat_axis=0, tiled=...  7.33 us
    all_to_all x1, waiting for transfers between devices, local(): lax.all_to_all(request, ('gx', 'gy'), split_axis=0, concat_axis=0, tiled=...  4.11 us
    all_to_all x1, waiting for transfers between devices, local(): lax.all_to_all(present.reshape(part_count, capacity), ('gx', 'gy'), split...  3.68 us
    gather x2, local copies, waits for them, and re-layouts, local(): facets[lax.all_to_all(request, ('gx', 'gy'), split_axis=0, concat_axis=0,...  3.17 us
    all_to_all x1, starting transfers between devices, local(): lax.all_to_all(outgoing.reshape(part_count, capacity, 12, facet_width), (...  2.62 us
  transfers between devices with their start and end apart: 4, of which 4 were waited for; matrix products, arithmetic and copies ran while one was open for 16% of the time, Pallas kernels for 0%

commit v1 on v0

v1 whole, which is shorter than its diff:
```python
import functools

import jax
import jax.numpy as jnp
from jax import lax
from jax.experimental import pallas as pl
from jax.experimental.pallas import tpu as pltpu
from jax.sharding import PartitionSpec as P

CAP = 4
GC = 2
COMP = 4
LANES = 128

far_gap = 10.0
penalty = 1e30

MESH = pl.DeviceIdType.MESH


def split_terms(value):
    high = value.astype(jnp.bfloat16)
    rest = value - high.astype(jnp.float32)
    middle = rest.astype(jnp.bfloat16)
    low = (rest - middle.astype(jnp.float32)).astype(jnp.bfloat16)
    return high, middle, low


def facet_planes(planes):
    a, c, e, normal = (planes[0:3], planes[3:6], planes[6:9], planes[9:12])
    linear = [normal[i] - 2.0 * ((a[i] + c[i] + e[i]) / 3.0) for i in range(3)]
    spread = sum(a[i] * a[i] + c[i] * c[i] + e[i] * e[i] for i in range(3)) / 3.0
    offset = spread - sum(normal[i] * a[i] for i in range(3))
    return linear + [offset]


def lane_rows(row):
    return jnp.broadcast_to(row, (LANES, LANES)).T


def kernel(
    n_gx,
    n_gy,
    facets_ref,
    owner_ref,
    ghosts_ref,
    count_ref,
    nodes_ref,
    cand_ref,
    own_ref,
    ghost_ref,
    planes,
    own_send,
    own_recv,
    list_recv,
    reply_send,
    reply_recv,
    points,
    pens,
    entry_rows,
    own_acc,
    ghost_acc,
    load_sem,
    list_send_sem,
    list_recv_sem,
    own_send_sem,
    own_recv_sem,
    reply_send_sem,
    reply_recv_sem,
):
    n = n_gx * n_gy
    blocks = planes.shape[1]
    nodes = nodes_ref.shape[1]
    entries = ghosts_ref.shape[1]
    copies = LANES // blocks
    columns = COMP * blocks
    me = lax.axis_index("gx") * n_gy + lax.axis_index("gy")

    def coords(p):
        return (p // n_gy, p % n_gy)

    barrier = pltpu.get_barrier_semaphore()

    @pl.loop(1, n)
    def _(d):
        pl.semaphore_signal(
            barrier, inc=1, device_id=coords(lax.rem(me + d, n)), device_id_type=MESH
        )

    load = pltpu.make_async_copy(facets_ref, planes, load_sem)
    load.start()

    owner_row = jnp.concatenate([owner_ref[...]] * copies, axis=1)
    owner_col = lane_rows(owner_row)[0:blocks]
    lane = lax.broadcasted_iota(jnp.int32, (1, LANES), 1)
    place = lax.broadcasted_iota(jnp.int32, (blocks, LANES), 0)
    before = (owner_col == owner_row) & (place < lane % blocks)
    rank = jnp.sum(jnp.where(before, 1, 0), axis=0, keepdims=True)
    key = (owner_row * CAP + rank) * COMP + lane // blocks

    load.wait()
    features = facet_planes([planes[i] for i in range(12)])
    table = jnp.concatenate(features, axis=0)
    high, middle, low = split_terms(table)
    ones = jnp.ones((columns, LANES), jnp.bfloat16)
    stacked = jnp.concatenate([high, middle, low, ones], axis=1)

    tile = 128
    for start in range(0, n * CAP * COMP, tile):
        row = start + lax.broadcasted_iota(jnp.int32, (tile, LANES), 0)
        hot = jnp.concatenate(
            [jnp.where(row == key + i * copies, 1.0, 0.0) for i in range(COMP // copies)], axis=1
        ).astype(jnp.bfloat16)
        got = jnp.dot(hot, stacked, preferred_element_type=jnp.float32)
        value = got[:, 0:LANES] + got[:, LANES : 2 * LANES] + got[:, 2 * LANES : 3 * LANES]
        missing = (got[:, 3 * LANES :] == 0.0) & (row % COMP == COMP - 1)
        value = jnp.where(missing, penalty, value)
        per = tile // (CAP * COMP)
        own_send[start // (CAP * COMP) : start // (CAP * COMP) + per] = value.reshape(
            per, CAP * COMP, LANES
        )

    pl.semaphore_wait(barrier, n - 1)

    def list_copy(d):
        return pltpu.make_async_remote_copy(
            src_ref=ghosts_ref,
            dst_ref=list_recv.at[me],
            send_sem=list_send_sem,
            recv_sem=list_recv_sem,
            device_id=coords(lax.rem(me + d, n)),
            device_id_type=MESH,
        )

    def own_copy(d):
        target = lax.rem(me + d, n)
        return pltpu.make_async_remote_copy(
            src_ref=own_send.at[target],
            dst_ref=own_recv.at[me],
            send_sem=own_send_sem,
            recv_sem=own_recv_sem.at[me],
            device_id=coords(target),
            device_id_type=MESH,
        )

    def reply_copy(d):
        target = lax.rem(me + d, n)
        return pltpu.make_async_remote_copy(
            src_ref=reply_send.at[target],
            dst_ref=reply_recv.at[me],
            send_sem=reply_send_sem,
            recv_sem=reply_recv_sem,
            device_id=coords(target),
            device_id_type=MESH,
        )

    @pl.loop(1, n)
    def _(d):
        list_copy(d).start()

    @pl.loop(1, n)
    def _(d):
        own_copy(d).start()

    for start in range(0, nodes, LANES):
        rows = slice(start, start + LANES)
        for i in range(3):
            points[i, rows] = lane_rows(nodes_ref[i : i + 1, rows])
        chosen = [lane_rows(cand_ref[k : k + 1, rows]) for k in range(cand_ref.shape[0])]
        for e in range(entries):
            hit = functools.reduce(jnp.logical_or, [c == e for c in chosen])
            alive = jnp.where(e < count_ref[0], 0.0, penalty)
            pens[e, rows] = jnp.where(hit, alive, penalty)
    own_acc[...] = jnp.full(own_acc.shape, penalty, jnp.float32)

    wide = jnp.broadcast_to(ghosts_ref[...], (entries * COMP, entries))
    mine = lax.broadcasted_iota(jnp.int32, wide.shape, 1)
    rows_e = lax.broadcasted_iota(jnp.int32, wide.shape, 0)
    chosen_id = jnp.sum(jnp.where(mine == rows_e // COMP, wide, 0), axis=1, keepdims=True)
    holder = chosen_id // blocks
    larger = (wide // blocks == holder) & (wide > chosen_id)
    second = jnp.max(jnp.where(larger, 1, 0), axis=1, keepdims=True)
    component = lax.broadcasted_iota(jnp.int32, second.shape, 0) % COMP
    entry_rows[...] = jnp.broadcast_to(
        (holder * GC + second) * COMP + component, entry_rows.shape
    )

    list_recv[me] = ghosts_ref[...]
    pltpu.make_async_copy(
        list_recv.at[pl.ds(0, n - 1)], list_recv.at[pl.ds(0, n - 1)], list_recv_sem
    ).wait()
    group = 16
    for start in range(0, n, group):
        wanted = jnp.broadcast_to(list_recv[start : start + group], (group, 8, entries))
        local = wanted - me * blocks
        here = (local >= 0) & (local < blocks)
        far = 1 << 20
        first = jnp.max(jnp.where(here, local, -far), axis=2, keepdims=True)
        last = jnp.min(jnp.where(here, local, far), axis=2, keepdims=True)
        sub = lax.broadcasted_iota(jnp.int32, first.shape, 1)
        pick = jnp.where(sub < COMP, first, last) + (sub % COMP) * blocks
        pick = jnp.broadcast_to(pick, (group, 8, columns)).reshape(group * 8, columns)
        hot = jnp.where(
            pick == lax.broadcasted_iota(jnp.int32, (group * 8, columns), 1), 1.0, 0.0
        ).astype(jnp.bfloat16)
        got = jnp.dot(hot, stacked[:, 0 : 3 * LANES], preferred_element_type=jnp.float32)
        value = got[:, 0:LANES] + got[:, LANES : 2 * LANES] + got[:, 2 * LANES : 3 * LANES]
        reply_send[start : start + group] = value.reshape(group, 8, LANES)

    @pl.loop(1, n)
    def _(d):
        reply_copy(d).start()

    reply_recv[me] = reply_send[me]
    own_recv[me] = own_send[me]

    step = 64

    def own_chunk(source):
        chunk = own_recv[source]
        parts = [[chunk[COMP * c + k : COMP * c + k + 1] for k in range(COMP)] for c in range(CAP)]
        for start in range(0, nodes, step):
            rows = slice(start, start + step)
            x, y, z = points[0, rows], points[1, rows], points[2, rows]
            best = own_acc[rows]
            for lx, ly, lz, offset in parts:
                best = jnp.minimum(best, (x * lx + offset) + (y * ly + z * lz))
            own_acc[rows] = best

    own_chunk(me)

    @pl.loop(1, n)
    def _(d):
        source = lax.rem(me + n - d, n)
        pltpu.make_async_copy(
            own_recv.at[source], own_recv.at[source], own_recv_sem.at[source]
        ).wait()
        own_chunk(source)

    square = jnp.sum(nodes_ref[...] * nodes_ref[...], axis=0, keepdims=True)
    for start in range(0, nodes, LANES):
        rows = slice(start, start + LANES)
        least = jnp.min(own_acc[rows].T, axis=0, keepdims=True)
        own_ref[:, rows] = least + square[:, rows]

    pltpu.make_async_copy(
        reply_recv.at[pl.ds(0, n - 1)], reply_recv.at[pl.ds(0, n - 1)], reply_recv_sem
    ).wait()
    reply = reply_recv[...].reshape(n * GC * COMP, LANES)
    spot = lax.broadcasted_iota(jnp.int32, (entries * COMP, n * GC * COMP), 1)
    target_row = jnp.broadcast_to(entry_rows[:, 0:1], spot.shape)
    hot = jnp.where(target_row == spot, 1.0, 0.0).astype(jnp.bfloat16)
    got = jnp.dot(
        hot, jnp.concatenate(split_terms(reply), axis=1), preferred_element_type=jnp.float32
    )
    fetched = got[:, 0:LANES] + got[:, LANES : 2 * LANES] + got[:, 2 * LANES : 3 * LANES]
    ghost_acc[...] = fetched
    for start in range(0, nodes, LANES):
        bests = []
        for inner in range(start, start + LANES, 32):
            rows = slice(inner, inner + 32)
            x, y, z = points[0, rows], points[1, rows], points[2, rows]
            best = jnp.full((32, LANES), penalty, jnp.float32)
            for e in range(entries):
                lx, ly, lz, offset = [
                    ghost_acc[COMP * e + k : COMP * e + k + 1] for k in range(COMP)
                ]
                gap = (x * lx + offset) + (y * ly + z * lz)
                best = jnp.minimum(best, gap + pens[e, rows])
            bests.append(best)
        rows = slice(start, start + LANES)
        least = jnp.min(jnp.concatenate(bests, axis=0).T, axis=0, keepdims=True)
        ghost_ref[:, rows] = jnp.minimum(far_gap, least + square[:, rows])

    def all_of(ref, sem):
        pltpu.make_async_copy(ref.at[pl.ds(0, n - 1)], ref.at[pl.ds(0, n - 1)], sem).wait()

    all_of(list_recv, list_send_sem)
    all_of(own_recv, own_send_sem)
    all_of(reply_recv, reply_send_sem)


def solution(mesh):
    n_gx, n_gy = mesh.shape["gx"], mesh.shape["gy"]
    n = n_gx * n_gy

    def local(facets, owner, ghosts, ghost_count, nodes, cand):
        blocks, width = facets.shape[0], facets.shape[2]
        node_count = nodes.shape[1]
        entries = ghosts.shape[1]
        vmem = pl.BlockSpec(memory_space=pltpu.VMEM)
        own, ghost = pl.pallas_call(
            functools.partial(kernel, n_gx, n_gy),
            out_shape=[jax.ShapeDtypeStruct((1, node_count), jnp.float32)] * 2,
            in_specs=[
                pl.BlockSpec(memory_space=pl.ANY),
                vmem,
                vmem,
                pl.BlockSpec(memory_space=pltpu.SMEM),
                vmem,
                vmem,
            ],
            out_specs=[vmem, vmem],
            scratch_shapes=[
                pltpu.VMEM((12, blocks, width), jnp.float32),
                pltpu.VMEM((n, CAP * COMP, width), jnp.float32),
                pltpu.VMEM((n, CAP * COMP, width), jnp.float32),
                pltpu.VMEM((n, 1, entries), jnp.int32),
                pltpu.VMEM((n, GC * COMP, width), jnp.float32),
                pltpu.VMEM((n, GC * COMP, width), jnp.float32),
                pltpu.VMEM((3, node_count, width), jnp.float32),
                pltpu.VMEM((entries, node_count, width), jnp.float32),
                pltpu.VMEM((entries * COMP, width), jnp.int32),
                pltpu.VMEM((node_count, width), jnp.float32),
                pltpu.VMEM((entries * COMP, width), jnp.float32),
                pltpu.SemaphoreType.DMA,
                pltpu.SemaphoreType.DMA,
                pltpu.SemaphoreType.DMA,
                pltpu.SemaphoreType.DMA,
                pltpu.SemaphoreType.DMA((n,)),
                pltpu.SemaphoreType.DMA,
                pltpu.SemaphoreType.DMA,
            ],
            compiler_params=pltpu.CompilerParams(collective_id=0, has_side_effects=True),
        )(
            jnp.transpose(facets, (1, 0, 2)),
            owner.reshape(1, blocks),
            ghosts,
            ghost_count,
            nodes,
            cand,
        )
        return own.reshape(node_count), ghost.reshape(node_count)

    return jax.shard_map(
        local,
        mesh=mesh,
        in_specs=(
            P(("gx", "gy"), None, None),
            P(("gx", "gy"), None),
            P(("gx", "gy"), None),
            P(("gx", "gy")),
            P(None, ("gx", "gy")),
            P(None, ("gx", "gy")),
        ),
        out_specs=(P(("gx", "gy")), P(("gx", "gy"))),
        check_vma=False,
    )
```

time: 99.7 us -> 26.2 us (0.26)
  waiting for transfers between devices: 32.6 us -> 0 us
  matrix products: 32.4 us -> 0 us
  Pallas kernels: 0 us -> 22.8 us
  starting transfers between devices: 15.1 us -> 0 us
  local copies, waits for them, and re-layouts: 12.1 us -> 1.89 us
  other arithmetic: 5.25 us -> 0 us
    all_to_all x4 -> x0, waiting for transfers between devices: 32.6 us -> none  [the longest x1 16.3 us: local(): lax.all_to_all(outgoing.reshape(part_count, capacity, 12, facet_width), (...]
    dot_general x5 -> x0, matrix products: 32.4 us -> none  [pair_gaps(): lax.dot_general(node_feat, facet_feat, (((0,), (0,)), ((), ())), precisio...]
    pallas_call x0 -> x1, Pallas kernels: none -> 22.8 us  [local(): pl.pallas_call(functools.partial(kernel, n_gx, n_gy), out_shape=[jax.Shap...]
    all_to_all x4 -> x0, starting transfers between devices: 15.1 us -> none  [the longest x1 7.33 us: local(): lax.all_to_all(request, ('gx', 'gy'), split_axis=0, concat_axis=0, tiled=...]
    gather x3 -> x0, local copies, waits for them, and re-layouts: 3.77 us -> none  [the longest x2 3.17 us: local(): facets[lax.all_to_all(request, ('gx', 'gy'), split_axis=0, concat_axis=0,...]
    scatter x2 -> x0, local copies, waits for them, and re-layouts: 3.21 us -> none  [the longest x1 2.44 us: local(): jnp.zeros((slot_count, 12, facet_width), jnp.float32).at[slot_of]]
    reduce_sum x9 -> x0, other arithmetic: 1.84 us -> none  [the longest x1 0.91 us: local(): rank_in = jnp.sum(before.astype(jnp.int32), axis=1, dtype=jnp.int32)]
    all_to_all x5 -> x0, local copies, waits for them, and re-layouts: 1.72 us -> none  [the longest x2 0.77 us: local(): lax.all_to_all(request, ('gx', 'gy'), split_axis=0, concat_axis=0, tiled=...]
  transfers between devices with their start and end apart: 4 -> 0, of which waited for: 4 -> 0; matrix products, arithmetic and copies ran while one was open for 16% -> 0% of each run, Pallas kernels for 0% -> 0%
where the time goes in v1:
time: 26.2 us; the launch traced here: 25.9 us
  Pallas kernels  22.8 us (87%)
  local copies, waits for them, and re-layouts  1.89 us (7%)
  between operations  1.29 us (5%)
    pallas_call x1, Pallas kernels, local(): pl.pallas_call(functools.partial(kernel, n_gx, n_gy), out_shape=[jax.Shap...  22.8 us
    unnamed x6, local copies, waits for them, and re-layouts  1.89 us

profile of v1, /device:TPU:0, one launch (start us, length us, event | category | flops | bytes accessed | tf_op | source)
XLA Modules:
  0.0 25.9 jit_solution(7358434430338796344)
XLA Ops:
  1.3 22.8 %shard_map.77 = (f32[1,512]{1,0:T(1,128)}, f32[1,512]{1,0:T(1,128)}) custom-call(f32[12,64,128]{2,1,0:T(8,128)} %bitcast.4, s32[1,64]{1,0:T(1,128)} %bitcast.7, s32[1,16]{1,0:T(1,128)} %ghosts_ref.1, s32[1]{0:T(128)S(6)} %copy.10.count_ref, f32[3,512]{1,0:T(4,128)} %nodes_ref.1, s32[4,512]{1,0:T(4,128)} %cand_ref.1), custom_call_target="tpu_custom_call" | custom-call | tf_op jit(solution)/shard_map/pallas_call | solution.py:292
  24.0 0.0 copy-start.1
  24.1 0.7 %copy-done.1 = f32[1,512]{1,0:T(1,128)S(1)} copy-done((f32[1,512]{1,0:T(1,128)S(1)}, f32[1,512]{1,0:T(1,128)}, u32[]{:S(2)}) %copy-start.1) | copy-done | bytes 2072
  24.7 0.0 copy-start
  24.7 0.6 %copy.11 = f32[512]{0:T(512)} copy(f32[512]{0:T(512)S(1)} %bitcast.6) | data formatting | bytes 4096
  25.3 0.1 copy-done
  25.4 0.6 %copy.12 = f32[512]{0:T(512)} copy(f32[512]{0:T(512)S(1)} %bitcast.5) | data formatting | bytes 4096
Async XLA Ops:
  24.0 0.7 %copy-start.1 = (f32[1,512]{1,0:T(1,128)S(1)}, f32[1,512]{1,0:T(1,128)}, u32[]{:S(2)}) copy-start(f32[1,512]{1,0:T(1,128)} %get-tuple-element.4) | copy-start | bytes 6148
  24.7 0.7 %copy-start = (f32[1,512]{1,0:T(1,128)S(1)}, f32[1,512]{1,0:T(1,128)}, u32[]{:S(2)}) copy-start(f32[1,512]{1,0:T(1,128)} %get-tuple-element.5) | copy-start | bytes 6148

commit v2 on v1

--- a/solution.py
+++ b/solution.py
@@ -41,15 +41,20 @@
 def kernel(
     n_gx,
     n_gy,
-    facets_ref,
+    facets_hbm,
+    owner_hbm,
+    ghosts_hbm,
+    count_hbm,
+    nodes_hbm,
+    cand_hbm,
+    own_ref,
+    ghost_ref,
+    planes,
     owner_ref,
     ghosts_ref,
     count_ref,
     nodes_ref,
     cand_ref,
-    own_ref,
-    ghost_ref,
-    planes,
     own_send,
     own_recv,
     list_recv,
@@ -74,21 +79,89 @@
     entries = ghosts_ref.shape[1]
     copies = LANES // blocks
     columns = COMP * blocks
-    me = lax.axis_index("gx") * n_gy + lax.axis_index("gy")
-
-    def coords(p):
-        return (p // n_gy, p % n_gy)
+    my_x, my_y = lax.axis_index("gx"), lax.axis_index("gy")
+    me = my_x * n_gy + my_y
+    pair = 2 if n_gy % 2 == 0 else 1
+    pairs = n_gy // pair
+    my_pair, my_side = lax.div(my_y, pair), lax.rem(my_y, pair)
+
+    def wrap(value, size):
+        value = jnp.where(value >= size, value - size, value)
+        return jnp.where(value < 0, value + size, value)
+
+    def peer(j, dx, flip, sign):
+        side = my_side if flip == 0 else pair - 1 - my_side
+        return wrap(my_x + sign * dx, n_gx), wrap(my_pair + sign * j, pairs) * pair + side
+
+    def near(body):
+        for flip in range(1, pair):
+            body(0, 0, flip)
+
+        @pl.loop(1, n_gx)
+        def _(dx):
+            for flip in range(pair):
+                body(0, dx, flip)
+
+    def far(body):
+        @pl.loop(1, pairs)
+        def _(j):
+            @pl.loop(0, n_gx)
+            def _(dx):
+                for flip in range(pair):
+                    body(j, dx, flip)
 
     barrier = pltpu.get_barrier_semaphore()
 
-    @pl.loop(1, n)
-    def _(d):
+    def greet(j, dx, flip):
         pl.semaphore_signal(
-            barrier, inc=1, device_id=coords(lax.rem(me + d, n)), device_id_type=MESH
+            barrier, inc=1, device_id=peer(j, dx, flip, 1), device_id_type=MESH
         )
 
-    load = pltpu.make_async_copy(facets_ref, planes, load_sem)
+    far(greet)
+    near(greet)
+
+    load = pltpu.make_async_copy(facets_hbm, planes, load_sem.at[0])
+    small = [
+        pltpu.make_async_copy(source, target, load_sem.at[1 + i])
+        for i, (source, target) in enumerate(
+            [
+                (owner_hbm, owner_ref),
+                (ghosts_hbm, ghosts_ref),
+                (count_hbm, count_ref),
+                (nodes_hbm, nodes_ref),
+                (cand_hbm, cand_ref),
+            ]
+        )
+    ]
+    for copy in small:
+        copy.start()
     load.start()
+    for copy in small:
+        copy.wait()
+
+    count = count_ref[...]
+    for start in range(0, nodes, LANES):
+        rows = slice(start, start + LANES)
+        for i in range(3):
+            points[i, rows] = lane_rows(nodes_ref[i : i + 1, rows])
+        chosen = [lane_rows(cand_ref[k : k + 1, rows]) for k in range(cand_ref.shape[0])]
+        for e in range(entries):
+            hit = functools.reduce(jnp.logical_or, [c == e for c in chosen])
+            alive = jnp.where(e < count, 0.0, penalty)
+            pens[e, rows] = jnp.where(hit, alive, penalty)
+    own_acc[...] = jnp.full(own_acc.shape, penalty, jnp.float32)
+
+    wide = jnp.broadcast_to(ghosts_ref[...], (entries * COMP, entries))
+    mine = lax.broadcasted_iota(jnp.int32, wide.shape, 1)
+    rows_e = lax.broadcasted_iota(jnp.int32, wide.shape, 0)
+    chosen_id = jnp.sum(jnp.where(mine == rows_e // COMP, wide, 0), axis=1, keepdims=True)
+    holder = chosen_id // blocks
+    larger = (wide // blocks == holder) & (wide > chosen_id)
+    second = jnp.max(jnp.where(larger, 1, 0), axis=1, keepdims=True)
+    component = lax.broadcasted_iota(jnp.int32, second.shape, 0) % COMP
+    entry_rows[...] = jnp.broadcast_to(
+        (holder * GC + second) * COMP + component, entry_rows.shape
+    )
 
     owner_row = jnp.concatenate([owner_ref[...]] * copies, axis=1)
     owner_col = lane_rows(owner_row)[0:blocks]
@@ -122,97 +195,28 @@
 
     pl.semaphore_wait(barrier, n - 1)
 
-    def list_copy(d):
-        return pltpu.make_async_remote_copy(
-            src_ref=ghosts_ref,
-            dst_ref=list_recv.at[me],
-            send_sem=list_send_sem,
-            recv_sem=list_recv_sem,
-            device_id=coords(lax.rem(me + d, n)),
-            device_id_type=MESH,
-        )
-
-    def own_copy(d):
-        target = lax.rem(me + d, n)
-        return pltpu.make_async_remote_copy(
-            src_ref=own_send.at[target],
-            dst_ref=own_recv.at[me],
-            send_sem=own_send_sem,
-            recv_sem=own_recv_sem.at[me],
-            device_id=coords(target),
-            device_id_type=MESH,
-        )
-
-    def reply_copy(d):
-        target = lax.rem(me + d, n)
-        return pltpu.make_async_remote_copy(
-            src_ref=reply_send.at[target],
-            dst_ref=reply_recv.at[me],
-            send_sem=reply_send_sem,
-            recv_sem=reply_recv_sem,
-            device_id=coords(target),
-            device_id_type=MESH,
-        )
-
-    @pl.loop(1, n)
-    def _(d):
-        list_copy(d).start()
-
-    @pl.loop(1, n)
-    def _(d):
-        own_copy(d).start()
-
-    for start in range(0, nodes, LANES):
-        rows = slice(start, start + LANES)
-        for i in range(3):
-            points[i, rows] = lane_rows(nodes_ref[i : i + 1, rows])
-        chosen = [lane_rows(cand_ref[k : k + 1, rows]) for k in range(cand_ref.shape[0])]
-        for e in range(entries):
-            hit = functools.reduce(jnp.logical_or, [c == e for c in chosen])
-            alive = jnp.where(e < count_ref[0], 0.0, penalty)
-            pens[e, rows] = jnp.where(hit, alive, penalty)
-    own_acc[...] = jnp.full(own_acc.shape, penalty, jnp.float32)
-
-    wide = jnp.broadcast_to(ghosts_ref[...], (entries * COMP, entries))
-    mine = lax.broadcasted_iota(jnp.int32, wide.shape, 1)
-    rows_e = lax.broadcasted_iota(jnp.int32, wide.shape, 0)
-    chosen_id = jnp.sum(jnp.where(mine == rows_e // COMP, wide, 0), axis=1, keepdims=True)
-    holder = chosen_id // blocks
-    larger = (wide // blocks == holder) & (wide > chosen_id)
-    second = jnp.max(jnp.where(larger, 1, 0), axis=1, keepdims=True)
-    component = lax.broadcasted_iota(jnp.int32, second.shape, 0) % COMP
-    entry_rows[...] = jnp.broadcast_to(
-        (holder * GC + second) * COMP + component, entry_rows.shape
-    )
-
-    list_recv[me] = ghosts_ref[...]
-    pltpu.make_async_copy(
-        list_recv.at[pl.ds(0, n - 1)], list_recv.at[pl.ds(0, n - 1)], list_recv_sem
-    ).wait()
-    group = 16
-    for start in range(0, n, group):
-        wanted = jnp.broadcast_to(list_recv[start : start + group], (group, 8, entries))
-        local = wanted - me * blocks
-        here = (local >= 0) & (local < blocks)
-        far = 1 << 20
-        first = jnp.max(jnp.where(here, local, -far), axis=2, keepdims=True)
-        last = jnp.min(jnp.where(here, local, far), axis=2, keepdims=True)
-        sub = lax.broadcasted_iota(jnp.int32, first.shape, 1)
-        pick = jnp.where(sub < COMP, first, last) + (sub % COMP) * blocks
-        pick = jnp.broadcast_to(pick, (group, 8, columns)).reshape(group * 8, columns)
-        hot = jnp.where(
-            pick == lax.broadcasted_iota(jnp.int32, (group * 8, columns), 1), 1.0, 0.0
-        ).astype(jnp.bfloat16)
-        got = jnp.dot(hot, stacked[:, 0 : 3 * LANES], preferred_element_type=jnp.float32)
-        value = got[:, 0:LANES] + got[:, LANES : 2 * LANES] + got[:, 2 * LANES : 3 * LANES]
-        reply_send[start : start + group] = value.reshape(group, 8, LANES)
-
-    @pl.loop(1, n)
-    def _(d):
-        reply_copy(d).start()
-
-    reply_recv[me] = reply_send[me]
-    own_recv[me] = own_send[me]
+    def send(source, target, send_sem, recv_sem):
+        def start(j, dx, flip):
+            to_x, to_y = peer(j, dx, flip, 1)
+            pltpu.make_async_remote_copy(
+                src_ref=source(to_x * n_gy + to_y),
+                dst_ref=target.at[me],
+                send_sem=send_sem,
+                recv_sem=recv_sem,
+                device_id=(to_x, to_y),
+                device_id_type=MESH,
+            ).start()
+
+        return start
+
+    list_start = send(lambda p: ghosts_ref, list_recv, list_send_sem, list_recv_sem)
+    own_start = send(lambda p: own_send.at[p], own_recv, own_send_sem, own_recv_sem.at[me])
+    reply_start = send(lambda p: reply_send.at[p], reply_recv, reply_send_sem, reply_recv_sem)
+
+    far(list_start)
+    near(list_start)
+    near(own_start)
+    far(own_start)
 
     step = 64
 
@@ -227,21 +231,49 @@
                 best = jnp.minimum(best, (x * lx + offset) + (y * ly + z * lz))
             own_acc[rows] = best
 
-    own_chunk(me)
-
-    @pl.loop(1, n)
-    def _(d):
-        source = lax.rem(me + n - d, n)
+    def own_take(j, dx, flip):
+        from_x, from_y = peer(j, dx, flip, -1)
+        source = from_x * n_gy + from_y
         pltpu.make_async_copy(
             own_recv.at[source], own_recv.at[source], own_recv_sem.at[source]
         ).wait()
         own_chunk(source)
 
+    own_recv[me] = own_send[me]
+    own_chunk(me)
+    near(own_take)
+
+    list_recv[me] = ghosts_ref[...]
+    pltpu.make_async_copy(
+        list_recv.at[pl.ds(0, n - 1)], list_recv.at[pl.ds(0, n - 1)], list_recv_sem
+    ).wait()
+    group = 16
+    for start in range(0, n, group):
+        wanted = jnp.broadcast_to(list_recv[start : start + group], (group, 8, entries))
+        local = wanted - me * blocks
+        here = (local >= 0) & (local < blocks)
+        outside = 1 << 20
+        first = jnp.max(jnp.where(here, local, -outside), axis=2, keepdims=True)
+        last = jnp.min(jnp.where(here, local, outside), axis=2, keepdims=True)
+        sub = lax.broadcasted_iota(jnp.int32, first.shape, 1)
+        pick = jnp.where(sub < COMP, first, last) + (sub % COMP) * blocks
+        pick = jnp.broadcast_to(pick, (group, 8, columns)).reshape(group * 8, columns)
+        hot = jnp.where(
+            pick == lax.broadcasted_iota(jnp.int32, (group * 8, columns), 1), 1.0, 0.0
+        ).astype(jnp.bfloat16)
+        got = jnp.dot(hot, stacked[:, 0 : 3 * LANES], preferred_element_type=jnp.float32)
+        value = got[:, 0:LANES] + got[:, LANES : 2 * LANES] + got[:, 2 * LANES : 3 * LANES]
+        reply_send[start : start + group] = value.reshape(group, 8, LANES)
+
+    far(reply_start)
+    near(reply_start)
+    reply_recv[me] = reply_send[me]
+    far(own_take)
     square = jnp.sum(nodes_ref[...] * nodes_ref[...], axis=0, keepdims=True)
     for start in range(0, nodes, LANES):
         rows = slice(start, start + LANES)
         least = jnp.min(own_acc[rows].T, axis=0, keepdims=True)
-        own_ref[:, rows] = least + square[:, rows]
+        own_ref[rows] = (least + square[:, rows]).reshape(LANES)
 
     pltpu.make_async_copy(
         reply_recv.at[pl.ds(0, n - 1)], reply_recv.at[pl.ds(0, n - 1)], reply_recv_sem
@@ -270,7 +302,7 @@
             bests.append(best)
         rows = slice(start, start + LANES)
         least = jnp.min(jnp.concatenate(bests, axis=0).T, axis=0, keepdims=True)
-        ghost_ref[:, rows] = jnp.minimum(far_gap, least + square[:, rows])
+        ghost_ref[rows] = jnp.minimum(far_gap, least + square[:, rows]).reshape(LANES)
 
     def all_of(ref, sem):
         pltpu.make_async_copy(ref.at[pl.ds(0, n - 1)], ref.at[pl.ds(0, n - 1)], sem).wait()
@@ -291,18 +323,16 @@
         vmem = pl.BlockSpec(memory_space=pltpu.VMEM)
         own, ghost = pl.pallas_call(
             functools.partial(kernel, n_gx, n_gy),
-            out_shape=[jax.ShapeDtypeStruct((1, node_count), jnp.float32)] * 2,
-            in_specs=[
-                pl.BlockSpec(memory_space=pl.ANY),
-                vmem,
-                vmem,
-                pl.BlockSpec(memory_space=pltpu.SMEM),
-                vmem,
-                vmem,
-            ],
+            out_shape=[jax.ShapeDtypeStruct((node_count,), jnp.float32)] * 2,
+            in_specs=[pl.BlockSpec(memory_space=pl.ANY)] * 6,
             out_specs=[vmem, vmem],
             scratch_shapes=[
                 pltpu.VMEM((12, blocks, width), jnp.float32),
+                pltpu.VMEM((1, blocks), jnp.int32),
+                pltpu.VMEM((1, entries), jnp.int32),
+                pltpu.VMEM((1, 1), jnp.int32),
+                pltpu.VMEM((3, node_count), jnp.float32),
+                pltpu.VMEM((cand.shape[0], node_count), jnp.int32),
                 pltpu.VMEM((n, CAP * COMP, width), jnp.float32),
                 pltpu.VMEM((n, CAP * COMP, width), jnp.float32),
                 pltpu.VMEM((n, 1, entries), jnp.int32),
@@ -313,7 +343,7 @@
                 pltpu.VMEM((entries * COMP, width), jnp.int32),
                 pltpu.VMEM((node_count, width), jnp.float32),
                 pltpu.VMEM((entries * COMP, width), jnp.float32),
-                pltpu.SemaphoreType.DMA,
+                pltpu.SemaphoreType.DMA((6,)),
                 pltpu.SemaphoreType.DMA,
                 pltpu.SemaphoreType.DMA,
                 pltpu.SemaphoreType.DMA,
@@ -326,11 +356,11 @@
             jnp.transpose(facets, (1, 0, 2)),
             owner.reshape(1, blocks),
             ghosts,
-            ghost_count,
+            ghost_count.reshape(1, 1),
             nodes,
             cand,
         )
-        return own.reshape(node_count), ghost.reshape(node_count)
+        return own, ghost
 
     return jax.shard_map(
         local,

time: 26.2 us -> 24.6 us (0.939)
  Pallas kernels: 22.8 us -> 21.2 us
    pallas_call x1, Pallas kernels: 22.8 us -> 21.2 us  [local(): pl.pallas_call(functools.partial(kernel, n_gx, n_gy), out_shape=[jax.Shap...]
where the time goes in v2:
time: 24.6 us; the launch traced here: 24.4 us
  Pallas kernels  21.2 us (86%)
  local copies, waits for them, and re-layouts  1.89 us (8%)
  between operations  1.29 us (5%)
    pallas_call x1, Pallas kernels, local(): pl.pallas_call(functools.partial(kernel, n_gx, n_gy), out_shape=[jax.Shap...  21.2 us
    unnamed x6, local copies, waits for them, and re-layouts  1.89 us

profile of v2, /device:TPU:0, one launch (start us, length us, event | category | flops | bytes accessed | tf_op | source)
XLA Modules:
  0.0 24.4 jit_solution(4575991106357913491)
XLA Ops:
  1.3 21.2 %shard_map.77 = (f32[512]{0:T(512)}, f32[512]{0:T(512)}) custom-call(f32[12,64,128]{2,1,0:T(8,128)} %bitcast.4, s32[1,64]{1,0:T(1,128)} %bitcast.5, s32[1,16]{1,0:T(1,128)} %ghosts_hbm.1, s32[1,1]{1,0:T(1,128)} %bitcast.3.count_hbm, f32[3,512]{1,0:T(4,128)} %nodes_hbm.1, s32[4,512]{1,0:T(4,128)} %cand_hbm.1), custom_call_target="tpu_custom_call" | custom-call | tf_op jit(solution)/shard_map/pallas_call | solution.py:324
  22.5 0.0 copy-start.1
  22.5 0.7 %copy-done.1 = f32[512]{0:T(512)S(1)} copy-done((f32[512]{0:T(512)S(1)}, f32[512]{0:T(512)}, u32[]{:S(2)}) %copy-start.1) | copy-done | bytes 2072
  23.1 0.0 copy-start
  23.1 0.6 %copy.11 = f32[512]{0:T(512)} copy(f32[512]{0:T(512)S(1)} %copy-done.1) | data formatting | bytes 4096
  23.7 0.1 copy-done
  23.8 0.6 %copy.12 = f32[512]{0:T(512)} copy(f32[512]{0:T(512)S(1)} %copy-done) | data formatting | bytes 4096
Async XLA Ops:
  22.5 0.7 %copy-start.1 = (f32[512]{0:T(512)S(1)}, f32[512]{0:T(512)}, u32[]{:S(2)}) copy-start(f32[512]{0:T(512)} %get-tuple-element.4) | copy-start | bytes 6148
  23.1 0.7 %copy-start = (f32[512]{0:T(512)S(1)}, f32[512]{0:T(512)}, u32[]{:S(2)}) copy-start(f32[512]{0:T(512)} %get-tuple-element.5) | copy-start | bytes 6148

commit v3 on v2

--- a/solution.py
+++ b/solution.py
@@ -63,6 +63,7 @@
     points,
     pens,
     entry_rows,
+    ids_ref,
     own_acc,
     ghost_acc,
     load_sem,
@@ -127,6 +128,7 @@
             [
                 (owner_hbm, owner_ref),
                 (ghosts_hbm, ghosts_ref),
+                (ghosts_hbm, ids_ref),
                 (count_hbm, count_ref),
                 (nodes_hbm, nodes_ref),
                 (cand_hbm, cand_ref),
@@ -138,30 +140,6 @@
     load.start()
     for copy in small:
         copy.wait()
-
-    count = count_ref[...]
-    for start in range(0, nodes, LANES):
-        rows = slice(start, start + LANES)
-        for i in range(3):
-            points[i, rows] = lane_rows(nodes_ref[i : i + 1, rows])
-        chosen = [lane_rows(cand_ref[k : k + 1, rows]) for k in range(cand_ref.shape[0])]
-        for e in range(entries):
-            hit = functools.reduce(jnp.logical_or, [c == e for c in chosen])
-            alive = jnp.where(e < count, 0.0, penalty)
-            pens[e, rows] = jnp.where(hit, alive, penalty)
-    own_acc[...] = jnp.full(own_acc.shape, penalty, jnp.float32)
-
-    wide = jnp.broadcast_to(ghosts_ref[...], (entries * COMP, entries))
-    mine = lax.broadcasted_iota(jnp.int32, wide.shape, 1)
-    rows_e = lax.broadcasted_iota(jnp.int32, wide.shape, 0)
-    chosen_id = jnp.sum(jnp.where(mine == rows_e // COMP, wide, 0), axis=1, keepdims=True)
-    holder = chosen_id // blocks
-    larger = (wide // blocks == holder) & (wide > chosen_id)
-    second = jnp.max(jnp.where(larger, 1, 0), axis=1, keepdims=True)
-    component = lax.broadcasted_iota(jnp.int32, second.shape, 0) % COMP
-    entry_rows[...] = jnp.broadcast_to(
-        (holder * GC + second) * COMP + component, entry_rows.shape
-    )
 
     owner_row = jnp.concatenate([owner_ref[...]] * copies, axis=1)
     owner_col = lane_rows(owner_row)[0:blocks]
@@ -217,6 +195,26 @@
     near(list_start)
     near(own_start)
     far(own_start)
+
+    count = count_ref[0]
+    for start in range(0, nodes, LANES):
+        rows = slice(start, start + LANES)
+        for i in range(3):
+            points[i, rows] = lane_rows(nodes_ref[i : i + 1, rows])
+        chosen = [lane_rows(cand_ref[k : k + 1, rows]) for k in range(cand_ref.shape[0])]
+        for e in range(entries):
+            hit = functools.reduce(jnp.logical_or, [c == e for c in chosen])
+            alive = jnp.where(e < count, 0.0, penalty)
+            pens[e, rows] = jnp.where(hit, alive, penalty)
+    own_acc[...] = jnp.full(own_acc.shape, penalty, jnp.float32)
+
+    wide = jnp.broadcast_to(ghosts_ref[...], (entries * COMP, entries))
+    mine = lax.broadcasted_iota(jnp.int32, wide.shape, 1)
+    rows_e = lax.broadcasted_iota(jnp.int32, wide.shape, 0)
+    chosen_id = jnp.sum(jnp.where(mine == rows_e // COMP, wide, 0), axis=1, keepdims=True)
+    larger = (wide // blocks == chosen_id // blocks) & (wide > chosen_id)
+    second = jnp.max(jnp.where(larger, 1, 0), axis=1, keepdims=True)
+    entry_rows[...] = jnp.broadcast_to(second, entry_rows.shape)
 
     step = 64
 
@@ -278,15 +276,10 @@
     pltpu.make_async_copy(
         reply_recv.at[pl.ds(0, n - 1)], reply_recv.at[pl.ds(0, n - 1)], reply_recv_sem
     ).wait()
-    reply = reply_recv[...].reshape(n * GC * COMP, LANES)
-    spot = lax.broadcasted_iota(jnp.int32, (entries * COMP, n * GC * COMP), 1)
-    target_row = jnp.broadcast_to(entry_rows[:, 0:1], spot.shape)
-    hot = jnp.where(target_row == spot, 1.0, 0.0).astype(jnp.bfloat16)
-    got = jnp.dot(
-        hot, jnp.concatenate(split_terms(reply), axis=1), preferred_element_type=jnp.float32
-    )
-    fetched = got[:, 0:LANES] + got[:, LANES : 2 * LANES] + got[:, 2 * LANES : 3 * LANES]
-    ghost_acc[...] = fetched
+    for e in range(entries):
+        block = reply_recv[lax.div(ids_ref[0, e], blocks)]
+        rows = slice(COMP * e, COMP * e + COMP)
+        ghost_acc[rows] = jnp.where(entry_rows[rows] == 1, block[COMP:], block[0:COMP])
     for start in range(0, nodes, LANES):
         bests = []
         for inner in range(start, start + LANES, 32):
@@ -323,14 +316,14 @@
         vmem = pl.BlockSpec(memory_space=pltpu.VMEM)
         own, ghost = pl.pallas_call(
             functools.partial(kernel, n_gx, n_gy),
-            out_shape=[jax.ShapeDtypeStruct((node_count,), jnp.float32)] * 2,
+            out_shape=[pltpu.VMEM((node_count,), jnp.float32)] * 2,
             in_specs=[pl.BlockSpec(memory_space=pl.ANY)] * 6,
             out_specs=[vmem, vmem],
             scratch_shapes=[
                 pltpu.VMEM((12, blocks, width), jnp.float32),
                 pltpu.VMEM((1, blocks), jnp.int32),
                 pltpu.VMEM((1, entries), jnp.int32),
-                pltpu.VMEM((1, 1), jnp.int32),
+                pltpu.SMEM((1,), jnp.int32),
                 pltpu.VMEM((3, node_count), jnp.float32),
                 pltpu.VMEM((cand.shape[0], node_count), jnp.int32),
                 pltpu.VMEM((n, CAP * COMP, width), jnp.float32),
@@ -341,9 +334,10 @@
                 pltpu.VMEM((3, node_count, width), jnp.float32),
                 pltpu.VMEM((entries, node_count, width), jnp.float32),
                 pltpu.VMEM((entries * COMP, width), jnp.int32),
+                pltpu.SMEM((1, entries), jnp.int32),
                 pltpu.VMEM((node_count, width), jnp.float32),
                 pltpu.VMEM((entries * COMP, width), jnp.float32),
-                pltpu.SemaphoreType.DMA((6,)),
+                pltpu.SemaphoreType.DMA((7,)),
                 pltpu.SemaphoreType.DMA,
                 pltpu.SemaphoreType.DMA,
                 pltpu.SemaphoreType.DMA,
@@ -356,7 +350,7 @@
             jnp.transpose(facets, (1, 0, 2)),
             owner.reshape(1, blocks),
             ghosts,
-            ghost_count.reshape(1, 1),
+            ghost_count,
             nodes,
             cand,
         )

time: 24.6 us -> 22.5 us (0.915)
  Pallas kernels: 21.2 us -> 19.9 us
  local copies, waits for them, and re-layouts: 1.89 us -> 1.16 us
    pallas_call x1, Pallas kernels: 21.2 us -> 19.9 us  [local(): pl.pallas_call(functools.partial(kernel, n_gx, n_gy), out_shape=[pltpu.VM...]
    unnamed x6 -> x2, local copies, waits for them, and re-layouts: 1.89 us -> 1.16 us
where the time goes in v3:
time: 22.5 us; the launch traced here: 22.4 us
  Pallas kernels  19.9 us (88%)
  between operations  1.29 us (6%)
  local copies, waits for them, and re-layouts  1.16 us (5%)
    pallas_call x1, Pallas kernels, local(): pl.pallas_call(functools.partial(kernel, n_gx, n_gy), out_shape=[pltpu.VM...  19.9 us
    unnamed x2, local copies, waits for them, and re-layouts  1.16 us

profile of v3, /device:TPU:0, one launch (start us, length us, event | category | flops | bytes accessed | tf_op | source)
XLA Modules:
  0.0 22.4 jit_solution(8521573497837052348)
XLA Ops:
  1.3 19.9 %shard_map.77 = (f32[512]{0:T(512)S(1)}, f32[512]{0:T(512)S(1)}) custom-call(f32[12,64,128]{2,1,0:T(8,128)} %bitcast.2, s32[1,64]{1,0:T(1,128)} %bitcast.3, s32[1,16]{1,0:T(1,128)} %ghosts_hbm.1, s32[1]{0:T(128)S(6)} %copy.12.count_hbm, f32[3,512]{1,0:T(4,128)} %nodes_hbm.1, s32[4,512]{1,0:T(4,128)} %cand_hbm.1), custom_call_target="tpu_custom_call" | custom-call | tf_op jit(solution)/shard_map/pallas_call | solution.py:317
  21.2 0.6 %copy.10 = f32[512]{0:T(512)} copy(f32[512]{0:T(512)S(1)} %get-tuple-element.2) | data formatting | bytes 4096
  21.8 0.6 %copy.11 = f32[512]{0:T(512)} copy(f32[512]{0:T(512)S(1)} %get-tuple-element.3) | data formatting | bytes 4096

commit v4 on v3

--- a/solution.py
+++ b/solution.py
@@ -111,6 +111,13 @@
                 for flip in range(pair):
                     body(j, dx, flip)
 
+    def every(body):
+        for j in list(range(1, pairs)) + [0]:
+            for dx in range(n_gx):
+                for flip in range(pair):
+                    if j or dx or flip:
+                        body(j, dx, flip)
+
     barrier = pltpu.get_barrier_semaphore()
 
     def greet(j, dx, flip):
@@ -118,8 +125,7 @@
             barrier, inc=1, device_id=peer(j, dx, flip, 1), device_id_type=MESH
         )
 
-    far(greet)
-    near(greet)
+    every(greet)
 
     load = pltpu.make_async_copy(facets_hbm, planes, load_sem.at[0])
     small = [
@@ -191,10 +197,8 @@
     own_start = send(lambda p: own_send.at[p], own_recv, own_send_sem, own_recv_sem.at[me])
     reply_start = send(lambda p: reply_send.at[p], reply_recv, reply_send_sem, reply_recv_sem)
 
-    far(list_start)
-    near(list_start)
-    near(own_start)
-    far(own_start)
+    every(list_start)
+    every(own_start)
 
     count = count_ref[0]
     for start in range(0, nodes, LANES):
@@ -263,8 +267,7 @@
         value = got[:, 0:LANES] + got[:, LANES : 2 * LANES] + got[:, 2 * LANES : 3 * LANES]
         reply_send[start : start + group] = value.reshape(group, 8, LANES)
 
-    far(reply_start)
-    near(reply_start)
+    every(reply_start)
     reply_recv[me] = reply_send[me]
     far(own_take)
     square = jnp.sum(nodes_ref[...] * nodes_ref[...], axis=0, keepdims=True)

time: 22.5 us -> 22.3 us (level)
  no operation moved by 1% of the time
where the time goes in v4:
time: 22.3 us; the launch traced here: 22.1 us
  Pallas kernels  19.7 us (88%)
  between operations  1.29 us (6%)
  local copies, waits for them, and re-layouts  1.16 us (5%)
    pallas_call x1, Pallas kernels, local(): pl.pallas_call(functools.partial(kernel, n_gx, n_gy), out_shape=[pltpu.VM...  19.7 us
    unnamed x2, local copies, waits for them, and re-layouts  1.16 us

profile of v4, /device:TPU:0, one launch (start us, length us, event | category | flops | bytes accessed | tf_op | source)
XLA Modules:
  0.0 22.1 jit_solution(11827078685036673664)
XLA Ops:
  1.3 19.7 %shard_map.77 = (f32[512]{0:T(512)S(1)}, f32[512]{0:T(512)S(1)}) custom-call(f32[12,64,128]{2,1,0:T(8,128)} %bitcast.2, s32[1,64]{1,0:T(1,128)} %bitcast.3, s32[1,16]{1,0:T(1,128)} %ghosts_hbm.1, s32[1]{0:T(128)S(6)} %copy.12.count_hbm, f32[3,512]{1,0:T(4,128)} %nodes_hbm.1, s32[4,512]{1,0:T(4,128)} %cand_hbm.1), custom_call_target="tpu_custom_call" | custom-call | tf_op jit(solution)/shard_map/pallas_call | solution.py:320
  21.0 0.6 %copy.10 = f32[512]{0:T(512)} copy(f32[512]{0:T(512)S(1)} %get-tuple-element.2) | data formatting | bytes 4096
  21.6 0.6 %copy.11 = f32[512]{0:T(512)} copy(f32[512]{0:T(512)S(1)} %get-tuple-element.3) | data formatting | bytes 4096
